TPU v7x, 32 devices: a whole 2x2x4 slice. The times are simulated.
32 devices in a mesh: dp: 8 (over z, x), tensor: 4 (over y, core).
Axes of the slice: x: 2, y: 2, z: 4, core: 2. Of those that a mesh axis runs over, the one named last changes fastest.
Arguments:
- noise: float32 [32, 16, 256], P('dp'), may hold values from -6 to 6
- velocity: float32 [32, 16, 256], P('dp'), may hold values from -6 to 6
- times: float32 [32], P('dp'), may hold values from 0 to 1
- labels: int32 [32], P('dp'), may hold values from 0 to 999
- step_count: int32 [], replicated, may hold values from 1 to 20
- stem: float32 [3592, 768], P(None, 'dp'), may hold values from -0.5 to 0.5
- stem_first: float32 [3592, 768], P(None, 'dp'), may hold values from -0.00030517578 to 0.00030517578
- stem_second: float32 [3592, 768], P(None, 'dp'), may hold values from 2.0840002e-11 to 3.3344003e-10
- w_in: float32 [2, 768, 9984], P(None, 'dp', 'tensor'), may hold values from -0.21875 to 0.21875
- w_in_first: float32 [2, 768, 9984], P(None, 'dp', 'tensor'), may hold values from -0.00030517578 to 0.00030517578
- w_in_second: float32 [2, 768, 9984], P(None, 'dp', 'tensor'), may hold values from 2.0840002e-11 to 3.3344003e-10
- w_out: float32 [2, 3840, 768], P(None, 'tensor', 'dp'), may hold values from -0.4375 to 0.4375
- w_out_first: float32 [2, 3840, 768], P(None, 'tensor', 'dp'), may hold values from -0.00030517578 to 0.00030517578
- w_out_second: float32 [2, 3840, 768], P(None, 'tensor', 'dp'), may hold values from 2.0840002e-11 to 3.3344003e-10
Outputs:
- loss: float32 [], replicated
- grad_norm: float32 [], replicated
- stem_new: float32 [3592, 768], P(None, 'dp')
- stem_first_new: float32 [3592, 768], P(None, 'dp')
- stem_second_new: float32 [3592, 768], P(None, 'dp')
- stem_low: bfloat16 [3592, 768], P(None, 'dp')
- w_in_new: float32 [2, 768, 9984], P(None, 'dp', 'tensor')
- w_in_first_new: float32 [2, 768, 9984], P(None, 'dp', 'tensor')
- w_in_second_new: float32 [2, 768, 9984], P(None, 'dp', 'tensor')
- w_in_low: bfloat16 [2, 768, 9984], P(None, 'dp', 'tensor')
- w_out_new: float32 [2, 3840, 768], P(None, 'tensor', 'dp')
- w_out_first_new: float32 [2, 3840, 768], P(None, 'tensor', 'dp')
- w_out_second_new: float32 [2, 3840, 768], P(None, 'tensor', 'dp')
- w_out_low: bfloat16 [2, 3840, 768], P(None, 'tensor', 'dp')
All inputs are finite; a program needn't handle non-finite values.
Results may differ from a plain program's by a relative error of at most 0.0071.
Values may be sent and summed in bfloat16 or wider, within the bound.
A program may use at most 192 MiB of HBM per device.

v0:
```python
import math
import jax
import jax.numpy as jnp
from jax import lax
from jax.sharding import PartitionSpec as P

D = 768
H = 12
DH = 64
FF = 3072
CLASSES = 1000
PF = 16
FREQ = 256
GRID = 16
LAYERS = 2
NTOK = 256
CLIP_AT = 1.0
LEARN_RATE = 0.03
BETA_ONE = 0.9
BETA_TWO = 0.999
EPSILON = 1e-08
DECAY = 0.01


def matmul(left, right):
    return jnp.dot(left, right, preferred_element_type=jnp.float32)


def dot_left(left, right):
    return lax.dot_general(
        left, right, (((0,), (0,)), ((), ())), preferred_element_type=jnp.float32
    )


def dot_right(left, right):
    return lax.dot_general(
        left, right, (((1,), (1,)), ((), ())), preferred_element_type=jnp.float32
    )


def normalize(values):
    center = values - jnp.mean(values, axis=-1, keepdims=True)
    spread = jnp.mean(center * center, axis=-1, keepdims=True)
    return center * lax.rsqrt(spread + 1e-06)


def modulate(values, shift, scale):
    return normalize(values) * (1.0 + scale[:, None, :]) + shift[:, None, :]


def positions(grid, width):
    quarter = width // 4
    omega = 1.0 / 10000.0 ** (jnp.arange(quarter, dtype=jnp.float32) / quarter)
    angles = jnp.arange(grid, dtype=jnp.float32)[:, None] * omega[None, :]
    single = jnp.concatenate([jnp.sin(angles), jnp.cos(angles)], axis=1)
    rows_part = jnp.repeat(single, grid, axis=0)
    cols_part = jnp.tile(single, (grid, 1))
    return jnp.concatenate([rows_part, cols_part], axis=1)


def time_features(times, count):
    half = count // 2
    freqs = jnp.exp(-math.log(10000.0) * jnp.arange(half, dtype=jnp.float32) / half)
    angles = 1000.0 * times[:, None] * freqs[None, :]
    return jnp.concatenate([jnp.cos(angles), jnp.sin(angles)], axis=1)


def layout(width):
    parts = lax.axis_size("tensor")
    heads = H // parts
    return (heads, 3 * heads * DH, FF // parts, 6 * width // parts)


def fetch_layer(w_in, w_out, layer):
    return (
        lax.all_gather(w_in[layer].astype(jnp.bfloat16), "dp", axis=0, tiled=True),
        lax.all_gather(w_out[layer].astype(jnp.bfloat16), "dp", axis=1, tiled=True),
    )


def combine(partial_value):
    return lax.psum(partial_value.astype(jnp.bfloat16), "tensor").astype(jnp.float32)


def attention_scores(qkv):
    query, key = (qkv[:, :, :, 0], qkv[:, :, :, 1])
    return jnp.einsum("bnhe,bmhe->bhnm", query, key, preferred_element_type=jnp.float32) * DH ** (
        -0.5
    )


def layer_forward(state, cond_act, win_b, wout_b):
    batch, width = (state.shape[0], state.shape[2])
    heads, qcols, fcols, mcols = layout(width)
    mod_part = matmul(cond_act, win_b[:, qcols + fcols :]).astype(jnp.bfloat16)
    mod = lax.all_gather(mod_part, "tensor", axis=1, tiled=True).astype(jnp.float32)
    pieces = jnp.split(mod, 6, axis=1)
    x_attn = modulate(state, pieces[0], pieces[1]).astype(jnp.bfloat16)
    tokens = x_attn.shape[1]
    x_attn = x_attn.reshape(-1, width)
    qkv = matmul(x_attn, win_b[:, :qcols]).astype(jnp.bfloat16).reshape(batch, tokens, heads, 3, DH)
    scores = attention_scores(qkv)
    total = jax.nn.logsumexp(scores, axis=-1, keepdims=True)
    probs = jnp.exp(scores - total).astype(jnp.bfloat16)
    context = jnp.einsum(
        "bhnm,bmhe->bnhe", probs, qkv[:, :, :, 2], preferred_element_type=jnp.float32
    )
    context = context.astype(jnp.bfloat16).reshape(-1, heads * DH)
    attn = combine(matmul(context, wout_b[: heads * DH]).reshape(batch, tokens, width))
    mid = state + pieces[2][:, None, :] * attn
    x_mlp = modulate(mid, pieces[3], pieces[4]).astype(jnp.bfloat16).reshape(-1, width)
    pre = matmul(x_mlp, win_b[:, qcols : qcols + fcols])
    act = jax.nn.gelu(pre, approximate=True).astype(jnp.bfloat16)
    out = combine(matmul(act, wout_b[heads * DH :]).reshape(batch, tokens, width))
    kept = (state, mod, x_attn, qkv, total, context, attn, mid, x_mlp, pre, act, out)
    return (mid + pieces[5][:, None, :] * out, kept)


def layer_backward(grad, kept, cond_act, win_b, wout_b):
    state, mod, x_attn, qkv, total, context, attn, mid, x_mlp, pre, act, out = kept
    batch, width = (state.shape[0], state.shape[2])
    heads, qcols, fcols, mcols = layout(width)
    tokens = qkv.shape[1]
    pieces = jnp.split(mod, 6, axis=1)
    gate_mlp = jnp.sum(grad * out, axis=1)
    d_out = (pieces[5][:, None, :] * grad).astype(jnp.bfloat16).reshape(-1, width)
    g_fc2 = dot_left(act, d_out)
    d_act = dot_right(d_out, wout_b[heads * DH :])
    gelu_back = jax.vjp(lambda v: jax.nn.gelu(v, approximate=True), pre)[1]
    d_pre = gelu_back(d_act)[0].astype(jnp.bfloat16)
    g_fc1 = dot_left(x_mlp, d_pre)
    d_xmlp = combine(
        dot_right(d_pre, win_b[:, qcols : qcols + fcols]).reshape(batch, tokens, width)
    )
    d_mid, shift_mlp, scale_mlp = jax.vjp(modulate, mid, pieces[3], pieces[4])[1](d_xmlp)
    d_mid = d_mid + grad
    gate_attn = jnp.sum(d_mid * attn, axis=1)
    d_attn = (pieces[2][:, None, :] * d_mid).astype(jnp.bfloat16).reshape(-1, width)
    g_proj = dot_left(context, d_attn)
    d_context = (
        dot_right(d_attn, wout_b[: heads * DH])
        .astype(jnp.bfloat16)
        .reshape(batch, tokens, heads, DH)
    )
    query, key, value = (qkv[:, :, :, 0], qkv[:, :, :, 1], qkv[:, :, :, 2])
    weights_full = jnp.exp(attention_scores(qkv) - total)
    d_probs = jnp.einsum("bnhe,bmhe->bhnm", d_context, value, preferred_element_type=jnp.float32)
    d_value = jnp.einsum(
        "bhnm,bnhe->bmhe",
        weights_full.astype(jnp.bfloat16),
        d_context,
        preferred_element_type=jnp.float32,
    )
    inner = jnp.sum(d_probs * weights_full, axis=-1, keepdims=True)
    d_scores = (weights_full * (d_probs - inner)).astype(jnp.bfloat16)
    d_query = jnp.einsum(
        "bhnm,bmhe->bnhe", d_scores, key, preferred_element_type=jnp.float32
    ) * DH ** (-0.5)
    d_key = jnp.einsum(
        "bhnm,bnhe->bmhe", d_scores, query, preferred_element_type=jnp.float32
    ) * DH ** (-0.5)
    d_qkv = jnp.stack([d_query, d_key, d_value], axis=3).astype(jnp.bfloat16).reshape(-1, qcols)
    g_qkv = dot_left(x_attn, d_qkv)
    d_xattn = combine(dot_right(d_qkv, win_b[:, :qcols]).reshape(batch, tokens, width))
    d_state, shift_attn, scale_attn = jax.vjp(modulate, state, pieces[0], pieces[1])[1](d_xattn)
    d_state = d_state + d_mid
    d_mod = jnp.concatenate(
        [shift_attn, scale_attn, gate_attn, shift_mlp, scale_mlp, gate_mlp], axis=1
    )
    d_mod = lax.dynamic_slice_in_dim(d_mod, lax.axis_index("tensor") * mcols, mcols, 1)
    d_mod = d_mod.astype(jnp.bfloat16)
    g_mod = dot_left(cond_act, d_mod)
    d_cond = dot_right(d_mod, win_b[:, qcols + fcols :])
    return (
        d_state,
        d_cond,
        jnp.concatenate([g_qkv, g_fc1, g_mod], axis=1),
        jnp.concatenate([g_proj, g_fc2], axis=0),
    )


def adamw(weight, first, second, gradient, fix_one, fix_two):
    first = BETA_ONE * first + (1.0 - BETA_ONE) * gradient
    second = BETA_TWO * second + (1.0 - BETA_TWO) * gradient * gradient
    step = first / fix_one / (jnp.sqrt(second / fix_two) + EPSILON) + DECAY * weight
    fresh = weight - LEARN_RATE * step
    return (fresh, first, second, fresh.astype(jnp.bfloat16))


def on_device(
    noise,
    velocity,
    times,
    labels,
    step_count,
    stem,
    stem_first,
    stem_second,
    w_in,
    w_in_first,
    w_in_second,
    w_out,
    w_out_first,
    w_out_second,
):
    parts = lax.axis_size("tensor")
    batch = noise.shape[0]
    gathered = lax.all_gather(stem.astype(jnp.bfloat16), "dp", axis=1, tiled=True)
    offsets = [PF, PF + FREQ, PF + FREQ + D, PF + FREQ + D + CLASSES, PF + FREQ + 3 * D + CLASSES]
    patch, freq_w, time_w, table, final_mod, final_out = jnp.split(gathered, offsets, axis=0)
    tokens = (
        jnp.swapaxes(noise + times[:, None, None] * velocity, 1, 2)
        .reshape(-1, PF)
        .astype(jnp.bfloat16)
    )
    embed = matmul(tokens, patch).reshape(batch, NTOK, D) + positions(GRID, D)[None]
    features = time_features(times, FREQ).astype(jnp.bfloat16)
    time_pre = matmul(features, freq_w)
    hidden = jax.nn.silu(time_pre).astype(jnp.bfloat16)
    onehot = (labels[:, None] == jnp.arange(CLASSES, dtype=jnp.int32)[None, :]).astype(jnp.bfloat16)
    cond = matmul(hidden, time_w) + matmul(onehot, table)
    cond_act = jax.nn.silu(cond).astype(jnp.bfloat16)
    state = embed
    saved = []
    for layer in range(LAYERS):
        win_b, wout_b = fetch_layer(w_in, w_out, layer)
        state, kept = layer_forward(state, cond_act, win_b, wout_b)
        saved.append(kept)
    final = dot_right(cond_act, final_mod)
    x_final = modulate(state, final[:, :D], final[:, D:]).astype(jnp.bfloat16).reshape(-1, D)
    pred = dot_right(x_final, final_out).reshape(batch, NTOK, PF)
    diff = pred - jnp.swapaxes(velocity, 1, 2)
    weight_time = 0.5 + times
    loss_local = jnp.sum(weight_time * jnp.mean(diff * diff, axis=(1, 2)))
    d_pred = (
        (2.0 / (NTOK * PF) * weight_time[:, None, None] * diff).astype(jnp.bfloat16).reshape(-1, PF)
    )
    g_final_out = dot_left(d_pred, x_final)
    d_xfinal = matmul(d_pred, final_out).reshape(batch, NTOK, D)
    grad, final_shift, final_scale = jax.vjp(modulate, state, final[:, :D], final[:, D:])[1](
        d_xfinal
    )
    d_final = jnp.concatenate([final_shift, final_scale], axis=1).astype(jnp.bfloat16)
    g_final_mod = dot_left(d_final, cond_act)
    d_cond_final = matmul(d_final, final_mod)
    d_cond_layers = jnp.zeros((batch, D), jnp.float32)
    in_grads = [None] * LAYERS
    out_grads = [None] * LAYERS
    for layer in reversed(range(LAYERS)):
        win_b, wout_b = (
            lax.all_gather(w_in[layer].astype(jnp.bfloat16), "dp", axis=0, tiled=True),
            lax.all_gather(w_out[layer].astype(jnp.bfloat16), "dp", axis=1, tiled=True),
        )
        grad, d_part, g_in, g_outw = layer_backward(grad, saved[layer], cond_act, win_b, wout_b)
        d_cond_layers = d_cond_layers + d_part
        g_in, g_outw = (
            lax.psum_scatter(g_in, "dp", scatter_dimension=0, tiled=True),
            lax.psum_scatter(g_outw, "dp", scatter_dimension=1, tiled=True),
        )
        in_grads[layer] = g_in
        out_grads[layer] = g_outw
    d_cond_act = lax.psum(d_cond_layers, "tensor") + d_cond_final
    d_cond = jax.vjp(jax.nn.silu, cond)[1](d_cond_act)[0].astype(jnp.bfloat16)
    g_time = dot_left(hidden, d_cond)
    g_table = dot_left(onehot, d_cond)
    d_hidden = dot_right(d_cond, time_w)
    d_time_pre = jax.vjp(jax.nn.silu, time_pre)[1](d_hidden)[0].astype(jnp.bfloat16)
    g_freq = dot_left(features, d_time_pre)
    d_embed = grad.astype(jnp.bfloat16).reshape(-1, D)
    g_patch = dot_left(tokens, d_embed)
    stem_grad = jnp.concatenate(
        [g_patch, g_freq, g_time, g_table, g_final_mod, g_final_out], axis=0
    )
    stem_grad = lax.psum_scatter(stem_grad, "dp", scatter_dimension=1, tiled=True)
    in_stack = jnp.stack(in_grads)
    out_stack = jnp.stack(out_grads)
    squares = (
        jnp.sum(stem_grad * stem_grad) / parts
        + jnp.sum(in_stack * in_stack)
        + jnp.sum(out_stack * out_stack)
    )
    loss, square_total = lax.psum((loss_local / parts, squares), ("dp", "tensor"))
    grad_norm = jnp.sqrt(square_total)
    factor = jnp.minimum(1.0, CLIP_AT / grad_norm)
    steps_done = step_count.astype(jnp.float32)
    fix_one = 1.0 - jnp.power(BETA_ONE, steps_done)
    fix_two = 1.0 - jnp.power(BETA_TWO, steps_done)
    stem_out = adamw(stem, stem_first, stem_second, factor * stem_grad, fix_one, fix_two)
    in_out = adamw(w_in, w_in_first, w_in_second, factor * in_stack, fix_one, fix_two)
    out_out = adamw(w_out, w_out_first, w_out_second, factor * out_stack, fix_one, fix_two)
    return (
        loss,
        grad_norm,
        stem_out[0],
        stem_out[1],
        stem_out[2],
        stem_out[3],
        in_out[0],
        in_out[1],
        in_out[2],
        in_out[3],
        out_out[0],
        out_out[1],
        out_out[2],
        out_out[3],
    )


def solution(mesh):
    in_specs = (
        P("dp", None, None),
        P("dp", None, None),
        P("dp"),
        P("dp"),
        P(),
        P(None, "dp"),
        P(None, "dp"),
        P(None, "dp"),
        P(None, "dp", "tensor"),
        P(None, "dp", "tensor"),
        P(None, "dp", "tensor"),
        P(None, "tensor", "dp"),
        P(None, "tensor", "dp"),
        P(None, "tensor", "dp"),
    )
    out_specs = (
        P(),
        P(),
        P(None, "dp"),
        P(None, "dp"),
        P(None, "dp"),
        P(None, "dp"),
        P(None, "dp", "tensor"),
        P(None, "dp", "tensor"),
        P(None, "dp", "tensor"),
        P(None, "dp", "tensor"),
        P(None, "tensor", "dp"),
        P(None, "tensor", "dp"),
        P(None, "tensor", "dp"),
        P(None, "tensor", "dp"),
    )
    return jax.shard_map(
        on_device, mesh=mesh, in_specs=in_specs, out_specs=out_specs, check_vma=False
    )
```

profile of v0, /device:TPU:0, one launch (start us, length us, event | category | flops | bytes accessed | tf_op | source)
XLA Modules:
  0.0 1505.1 jit_solution(16987671061796512401)
XLA Ops:
  12.6 70.4 %all-gather.12.cloned.1.call-done = bf16[1,768,2496]{2,1,0:T(8,128)(2,1)} async-done(((bf16[1,96,2496]{2,1,0:T(8,128)(2,1)}), bf16[1,768,2496]{2,1,0:T(8,128)(2,1)}) %all-gather.12.cloned.1.call-update) | async-done | bytes 3833872 | tf_op jit(solution)/shard_map/all_gather | solution.py:76
  83.0 6.2 copy.167
  89.3 86.7 %all-gather.10.cloned.1.call-done = bf16[3592,768]{0,1:T(8,128)(2,1)} async-done(((bf16[3592,96]{0,1:T(8,128)(2,1)}), bf16[3592,768]{0,1:T(8,128)(2,1)}) %all-gather.10.cloned.1.call-update) | async-done | bytes 5517328 | tf_op jit(solution)/shard_map/all_gather | solution.py:208
  183.5 5.2 all_gather.27
  201.8 19.3 %all-gather.14.cloned.1.call-done = bf16[1,960,768]{1,2,0:T(8,128)(2,1)} async-done(((bf16[1,960,96]{1,2,0:T(8,128)(2,1)}), bf16[1,960,768]{1,2,0:T(8,128)(2,1)}) %all-gather.14.cloned.1.call-update) | async-done | bytes 1474576 | tf_op jit(solution)/shard_map/all_gather | solution.py:77
  224.7 40.6 %all-reduce.10.cloned.1.call-done = bf16[4,256,768]{2,1,0:T(8,128)(2,1)} async-done(((bf16[4,256,768]{2,1,0:T(8,128)(2,1)}), bf16[4,256,768]{2,1,0:T(8,128)(2,1)}) %all-reduce.10.cloned.1.call-update) | async-done | bytes 1572880 | tf_op jit(solution)/shard_map/psum | solution.py:82
  265.3 3.2 fusion.174
  270.8 3.3 fusion.81
  274.1 3.3 convolution_convert_fusion.8
  278.3 59.2 %all-gather.16.cloned.1.call-done = bf16[1,768,2496]{2,1,0:T(8,128)(2,1)} async-done(((bf16[1,96,2496]{2,1,0:T(8,128)(2,1)}), bf16[1,768,2496]{2,1,0:T(8,128)(2,1)}) %all-gather.16.cloned.1.call-update) | async-done | bytes 3833872 | tf_op jit(solution)/shard_map/all_gather | solution.py:76
  337.5 6.3 copy.173
  345.9 5.5 all_gather.30
  352.7 29.3 %all-reduce.12.cloned.1.call-done = bf16[4,256,768]{2,1,0:T(8,128)(2,1)} async-done(((bf16[4,256,768]{2,1,0:T(8,128)(2,1)}), bf16[4,256,768]{2,1,0:T(8,128)(2,1)}) %all-reduce.12.cloned.1.call-update) | async-done | bytes 1572880 | tf_op jit(solution)/shard_map/psum | solution.py:82
  387.1 3.3 convolution_convert_fusion.10
  390.3 3.5 reshape.360
  400.0 28.5 %all-gather.18.cloned.1.call-done = bf16[1,960,768]{1,2,0:T(8,128)(2,1)} async-done(((bf16[1,960,96]{1,2,0:T(8,128)(2,1)}), bf16[1,960,768]{1,2,0:T(8,128)(2,1)}) %all-gather.18.cloned.1.call-update) | async-done | bytes 1474576 | tf_op jit(solution)/shard_map/all_gather | solution.py:77
  431.4 41.3 %all-reduce.14.cloned.1.call-done = bf16[4,256,768]{2,1,0:T(8,128)(2,1)} async-done(((bf16[4,256,768]{2,1,0:T(8,128)(2,1)}), bf16[4,256,768]{2,1,0:T(8,128)(2,1)}) %all-reduce.14.cloned.1.call-update) | async-done | bytes 1572880 | tf_op jit(solution)/shard_map/psum | solution.py:82
  477.6 3.3 fusion.78
  481.0 3.3 convolution_convert_fusion.6
  488.0 39.4 %all-reduce.16.cloned.1.call-done = bf16[4,256,768]{2,1,0:T(8,128)(2,1)} async-done(((bf16[4,256,768]{2,1,0:T(8,128)(2,1)}), bf16[4,256,768]{2,1,0:T(8,128)(2,1)}) %all-reduce.16.cloned.1.call-update) | async-done | bytes 1572880 | tf_op jit(solution)/shard_map/psum | solution.py:82
  534.0 3.1 multiply_reduce_fusion
  542.5 3.7 fusion.33
  546.2 4.4 convolution_convert_fusion.5
  550.8 42.8 %all-reduce.18.cloned.1.call-done = bf16[4,256,768]{2,1,0:T(8,128)(2,1)} async-done(((bf16[4,256,768]{2,1,0:T(8,128)(2,1)}), bf16[4,256,768]{2,1,0:T(8,128)(2,1)}) %all-reduce.18.cloned.1.call-update) | async-done | bytes 1572880 | tf_op jit(solution)/shard_map/psum | solution.py:82
  593.7 3.2 fusion.11
  617.3 3.7 convolution_convert_fusion.3
  621.1 43.0 %all-reduce.20.cloned.1.call-done = bf16[4,256,768]{2,1,0:T(8,128)(2,1)} async-done(((bf16[4,256,768]{2,1,0:T(8,128)(2,1)}), bf16[4,256,768]{2,1,0:T(8,128)(2,1)}) %all-reduce.20.cloned.1.call-update) | async-done | bytes 1572880 | tf_op jit(solution)/shard_map/psum | solution.py:82
  664.1 3.2 fusion.10
  676.8 3.7 fusion.26
  680.5 4.4 convolution_convert_fusion.4
  687.3 40.7 %all-reduce.22.cloned.1.call-done = bf16[4,256,768]{2,1,0:T(8,128)(2,1)} async-done(((bf16[4,256,768]{2,1,0:T(8,128)(2,1)}), bf16[4,256,768]{2,1,0:T(8,128)(2,1)}) %all-reduce.22.cloned.1.call-update) | async-done | bytes 1572880 | tf_op jit(solution)/shard_map/psum | solution.py:82
  748.3 3.9 convolution_convert_fusion.2
  752.3 3.9 fusion.160
  760.6 3.9 fusion.159
  777.9 8.4 concatenate.43
  787.8 4.3 fusion.183
  803.4 9.5 concatenate.42
  816.7 11.1 psum.86
  830.6 4.0 fusion.65
  846.3 12.3 copy.221
  863.7 9.6 reduce-scatter.20.cloned.1.call-done
  874.4 75.6 %reduce-scatter.18.cloned.1.call-done = f32[96,960]{1,0:T(8,128)} async-done(((f32[768,960]{1,0:T(8,128)}), f32[96,960]{1,0:T(8,128)}) %reduce-scatter.18.cloned.1.call-update) | async-done | bytes 368656
  952.1 140.8 %reduce-scatter.14.cloned.1.call-done = f32[96,2496]{1,0:T(8,128)} async-done(((f32[768,2496]{1,0:T(8,128)}), f32[96,2496]{1,0:T(8,128)}) %reduce-scatter.14.cloned.1.call-update) | async-done | bytes 958480 | tf_op jit(solution)/shard_map/reduce_scatter | solution.py:257
  1092.8 142.8 %reduce-scatter.12.cloned.1.call-done = f32[96,2496]{1,0:T(8,128)} async-done(((f32[768,2496]{1,0:T(8,128)}), f32[96,2496]{1,0:T(8,128)}) %reduce-scatter.12.cloned.1.call-update) | async-done | bytes 958480 | tf_op jit(solution)/shard_map/reduce_scatter | solution.py:257
  1238.2 191.0 %reduce-scatter.16.cloned.1.call-done = f32[96,3592]{1,0:T(8,128)} async-done(((f32[768,3592]{1,0:T(8,128)}), f32[96,3592]{1,0:T(8,128)}) %reduce-scatter.16.cloned.1.call-update) | async-done | bytes 1379344
  1436.0 39.6 %all-reduce = (f32[]{:T(128)}, f32[]{:T(128)}) all-reduce(f32[]{:T(128)S(6)} %div.194, f32[]{:T(128)S(6)} %add.343), channel_id=1, replica_groups=mesh['dp'=8,'tensor'=4] {'dp','tensor'}, use_global_device_ids=true, to_apply=%region_20.21 | all-reduce | flops 2 | bytes 16 | tf_op jit(solution)/shard_map/psum | solution.py:282
  1476.3 3.6 fusion.161
  1487.0 6.9 fusion.163
  (537 shorter events, 195.4 us)
Async XLA Ops:
  7.2 75.8 %all-gather.12.cloned.1.call-start = ((), (), s32[]{:S(2)}) async-start(), calls=%async_computation.16 | async-start | bytes 4423680 | tf_op jit(solution)/shard_map/all_gather | solution.py:76
  10.0 165.9 %all-gather.10.cloned.1.call-start = ((), (), s32[]{:S(2)}) async-start(), calls=%async_computation.5 | async-start | bytes 6414336 | tf_op jit(solution)/shard_map/all_gather | solution.py:208
  11.1 210.0 %all-gather.14.cloned.1.call-start = ((), (), s32[]{:S(2)}) async-start(), calls=%async_computation.17 | async-start | bytes 1769472 | tf_op jit(solution)/shard_map/all_gather | solution.py:77
  12.0 253.3 %all-reduce.10.cloned.1.call-start = ((), (), s32[]{:S(2)}) async-start(), calls=%async_computation.6 | async-start | bytes 3145728 | tf_op jit(solution)/shard_map/psum | solution.py:82
  12.4 180.2 %copy-start.12 = (f32[256,768]{1,0:T(8,128)}, f32[256,768]{1,0:T(8,128)S(1)}, u32[]{:S(2)}) copy-start(f32[256,768]{1,0:T(8,128)S(1)} %pad_maximum_fusion.4) | copy-start | bytes 2359300
  12.5 176.8 %copy-start.104 = (bf16[4,256,16]{1,2,0:T(8,128)(2,1)}, bf16[4,256,16]{1,2,0:T(8,128)(2,1)S(1)}, u32[]{:S(2)}) copy-start(bf16[4,256,16]{1,2,0:T(8,128)(2,1)S(1)} %fusion.119) | copy-start | bytes 98308
  12.6 163.4 %copy-start.151 = (bf16[4,128]{1,0:T(4,128)(2,1)}, bf16[4,128]{1,0:T(4,128)(2,1)S(1)}, u32[]{:S(2)}) copy-start(bf16[4,128]{1,0:T(4,128)(2,1)S(1)} %get-tuple-element.143) | copy-start | bytes 3076
  12.6 163.4 %copy-start.153 = (bf16[4,128]{1,0:T(4,128)(2,1)}, bf16[4,128]{1,0:T(4,128)(2,1)S(1)}, u32[]{:S(2)}) copy-start(bf16[4,128]{1,0:T(4,128)(2,1)S(1)} %get-tuple-element.144) | copy-start | bytes 3076
  12.6 166.6 %copy-start.157 = (s32[4]{0:T(128)S(1)}, s32[4]{0:T(128)}, u32[]{:S(2)}) copy-start(s32[4]{0:T(128)} %param.17) | copy-start | bytes 52
  177.3 13.6 copy-start.106
  181.4 7.3 copy-start.92
  201.8 63.5 %copy-start.52 = (bf16[4,3,64,256]{3,2,1,0:T(8,128)(2,1)}, bf16[4,3,64,256]{3,2,1,0:T(8,128)(2,1)S(1)}, u32[]{:S(2)}) copy-start(bf16[4,3,64,256]{3,2,1,0:T(8,128)(2,1)S(1)} %convolution_convert_fusion.15) | copy-start | bytes 1179652
  223.9 113.6 %all-gather.16.cloned.1.call-start = ((), (), s32[]{:S(2)}) async-start(), calls=%async_computation.18 | async-start | bytes 4423680 | tf_op jit(solution)/shard_map/all_gather | solution.py:76
  224.5 157.5 %all-reduce.12.cloned.1.call-start = ((), (), s32[]{:S(2)}) async-start(), calls=%async_computation.7 | async-start | bytes 3145728 | tf_op jit(solution)/shard_map/psum | solution.py:82
  277.5 150.9 %all-gather.18.cloned.1.call-start = ((), (), s32[]{:S(2)}) async-start(), calls=%async_computation.19 | async-start | bytes 1769472 | tf_op jit(solution)/shard_map/all_gather | solution.py:77
  278.2 194.5 %all-reduce.14.cloned.1.call-start = ((), (), s32[]{:S(2)}) async-start(), calls=%async_computation.8 | async-start | bytes 3145728 | tf_op jit(solution)/shard_map/psum | solution.py:82
  431.3 96.1 %all-reduce.16.cloned.1.call-start = ((), (), s32[]{:S(2)}) async-start(), calls=%async_computation.9 | async-start | bytes 3145728 | tf_op jit(solution)/shard_map/psum | solution.py:82
  484.3 109.3 %all-reduce.18.cloned.1.call-start = ((), (), s32[]{:S(2)}) async-start(), calls=%async_computation.10 | async-start | bytes 3145728 | tf_op jit(solution)/shard_map/psum | solution.py:82
  530.2 6.8 copy-start.4
  530.3 6.8 copy-start.96
  530.8 6.3 copy-start.114
  540.0 6.1 copy-start.67
  550.6 113.5 %all-reduce.20.cloned.1.call-start = ((), (), s32[]{:S(2)}) async-start(), calls=%async_computation.11 | async-start | bytes 3145728 | tf_op jit(solution)/shard_map/psum | solution.py:82
  621.0 106.9 %all-reduce.22.cloned.1.call-start = ((), (), s32[]{:S(2)}) async-start(), calls=%async_computation.12 | async-start | bytes 3145728 | tf_op jit(solution)/shard_map/psum | solution.py:82
  672.7 7.8 copy-start.18
  673.0 7.5 copy-start.69
  684.9 111.3 %all-reduce.24.cloned.1.call-start = ((), (), s32[]{:S(2)}) async-start(), calls=%async_computation.13 | async-start | bytes 3145728 | tf_op jit(solution)/shard_map/psum | solution.py:82
  736.4 6.0 copy-start.9
  752.2 121.0 %reduce-scatter.20.cloned.1.call-start = ((), (), s32[]{:S(2)}) async-start(), calls=%async_computation.22 | async-start | bytes 3538944
  759.2 190.8 %reduce-scatter.18.cloned.1.call-start = ((), (), s32[]{:S(2)}) async-start(), calls=%async_computation.21 | async-start | bytes 3538944
  767.5 325.3 %reduce-scatter.14.cloned.1.call-start = ((), (), s32[]{:S(2)}) async-start(), calls=%async_computation.15 | async-start | bytes 8847360 | tf_op jit(solution)/shard_map/reduce_scatter | solution.py:257
  786.4 5.7 copy-start.31
  786.4 449.2 %reduce-scatter.12.cloned.1.call-start = ((), (), s32[]{:S(2)}) async-start(), calls=%async_computation.14 | async-start | bytes 8847360 | tf_op jit(solution)/shard_map/reduce_scatter | solution.py:257
  812.9 14.9 copy-start.138
  812.9 14.9 copy-start.139
  812.9 17.6 %copy-start.105 = (bf16[4,256,16]{1,2,0:T(8,128)(2,1)S(1)}, bf16[4,256,16]{1,2,0:T(8,128)(2,1)}, u32[]{:S(2)}) copy-start(bf16[4,256,16]{1,2,0:T(8,128)(2,1)} %copy-done.104) | copy-start | bytes 98308
  812.9 616.3 %reduce-scatter.16.cloned.1.call-start = ((), (), s32[]{:S(2)}) async-start(), calls=%async_computation.20 | async-start | bytes 12828672
  839.5 5.4 copy-start.5
  839.5 5.4 copy-start.75
  839.5 5.4 copy-start.83
  839.5 5.4 copy-start.97
  839.5 5.4 copy-start.109
  839.6 5.4 copy-start.115
  1479.9 7.1 copy-start.32
  1487.0 6.9 copy-start.39
  1487.0 6.9 copy-start.40
  1487.0 6.9 copy-start.71
  1487.0 6.9 copy-start.72
  (138 other events, 340.3 us)
Sparse Core Ops, SparseCore 0:
  10.8 72.1 all-gather.11
  85.8 90.1 all-gather.9
  178.7 42.3 all-gather.13
  224.0 41.2 all-reduce.9
  267.9 69.5 all-gather.15
  340.3 41.6 all-reduce.11
  384.2 44.2 all-gather.17
  431.5 41.2 all-reduce.13
  484.4 42.9 all-reduce.15
  550.7 42.8 all-reduce.17
  621.2 42.9 all-reduce.19
  685.0 42.8 all-reduce.21
  752.3 42.9 all-reduce.23
  798.7 74.4 reduce-scatter.19
  876.6 73.3 reduce-scatter.17
  953.5 139.2 reduce-scatter.13
  1096.3 139.2 reduce-scatter.11
  1239.2 189.9 reduce-scatter.15
where the time goes:
time: 1510 us
  waiting for transfers between devices  1100 us (73%)
  matrix products  130 us (9%)
  local copies, waits for them, and re-layouts  110 us (7%)
  other arithmetic  76.7 us (5%)
  blocking collectives  61.4 us (4%)
  between operations  21.8 us (1%)
    reduce_scatter x2, waiting for transfers between devices, on_device(): lax.psum_scatter(g_in, 'dp', scatter_dimension=0, tiled=True)  284 us
    unnamed x21, waiting for transfers between devices  278 us
    psum x8, waiting for transfers between devices, combine(): lax.psum(partial_value.astype(jnp.bfloat16), 'tensor').astype(jnp.float32)  277 us
    all_gather x2, waiting for transfers between devices, fetch_layer(): lax.all_gather(w_in[layer].astype(jnp.bfloat16), 'dp', axis=0, tiled=True)  130 us
    all_gather x1, waiting for transfers between devices, on_device(): lax.all_gather(stem.astype(jnp.bfloat16), 'dp', axis=1, tiled=True)  86.7 us
    unnamed x363, local copies, waits for them, and re-layouts  62.2 us
    all_gather x2, waiting for transfers between devices, fetch_layer(): lax.all_gather(w_out[layer].astype(jnp.bfloat16), 'dp', axis=1, tiled=True)  47.8 us
    dot_general x16, matrix products, matmul(): return jnp.dot(left, right, preferred_element_type=jnp.float32)  41.6 us
  transfers between devices with their start and end apart: 18, of which 17 were waited for; matrix products, arithmetic and copies ran while one was open for 11% of the time, Pallas kernels for 0%

commit v1 on v0

--- a/solution.py
+++ b/solution.py
@@ -22,6 +22,11 @@
 DECAY = 0.01
 
 
+def gather_and_add(x, axis):
+    parts = lax.all_gather(x, axis)
+    return jnp.sum(parts, axis=0)
+
+
 def matmul(left, right):
     return jnp.dot(left, right, preferred_element_type=jnp.float32)
 
@@ -79,7 +84,7 @@
 
 
 def combine(partial_value):
-    return lax.psum(partial_value.astype(jnp.bfloat16), "tensor").astype(jnp.float32)
+    return gather_and_add(partial_value.astype(jnp.bfloat16), "tensor").astype(jnp.float32)
 
 
 def attention_scores(qkv):

time: 1510 us -> 1570 us (1.040)
  other arithmetic: 76.7 us -> 119 us
    all_gather x0 -> x8, waiting for transfers between devices: none -> 303 us  [gather_and_add(): parts = lax.all_gather(x, axis)]
    psum x8 -> x0, waiting for transfers between devices: 277 us -> none  [combine(): lax.psum(partial_value.astype(jnp.bfloat16), 'tensor').astype(jnp.float32)]
    reduce_sum x0 -> x8, other arithmetic: none -> 42.7 us  [gather_and_add(): return jnp.sum(parts, axis=0)]
    unnamed x363 -> x365, local copies, waits for them, and re-layouts: 62.2 us -> 63.7 us
  transfers between devices with their start and end apart: 18 -> 18, of which waited for: 17 -> 18; matrix products, arithmetic and copies ran while one was open for 11% -> 11% of each run, Pallas kernels for 0% -> 0%
where the time goes in v1:
time: 1570 us; the launch traced here: 1560 us
  waiting for transfers between devices  1110 us (71%)
  matrix products  129 us (8%)
  other arithmetic  119 us (8%)
  local copies, waits for them, and re-layouts  110 us (7%)
  blocking collectives  61.8 us (4%)
  between operations  22.1 us (1%)
    all_gather x8, waiting for transfers between devices, gather_and_add(): parts = lax.all_gather(x, axis)  303 us
    reduce_scatter x2, waiting for transfers between devices, on_device(): lax.psum_scatter(g_in, 'dp', scatter_dimension=0, tiled=True)  284 us
    unnamed x21, waiting for transfers between devices  273 us
    all_gather x2, waiting for transfers between devices, fetch_layer(): lax.all_gather(w_in[layer].astype(jnp.bfloat16), 'dp', axis=0, tiled=True)  124 us
    all_gather x1, waiting for transfers between devices, on_device(): lax.all_gather(stem.astype(jnp.bfloat16), 'dp', axis=1, tiled=True)  86.7 us
    unnamed x365, local copies, waits for them, and re-layouts  63.7 us
    all_gather x2, waiting for transfers between devices, fetch_layer(): lax.all_gather(w_out[layer].astype(jnp.bfloat16), 'dp', axis=1, tiled=True)  44.1 us
    reduce_sum x8, other arithmetic, gather_and_add(): return jnp.sum(parts, axis=0)  42.7 us
  transfers between devices with their start and end apart: 18, of which 18 were waited for; matrix products, arithmetic and copies ran while one was open for 11% of the time, Pallas kernels for 0%

profile of v1, /device:TPU:0, one launch (start us, length us, event | category | flops | bytes accessed | tf_op | source)
XLA Modules:
  0.0 1559.4 jit_solution(16449888840358050372)
XLA Ops:
  12.6 70.4 %all-gather.32.cloned.1.call-done = bf16[1,768,2496]{2,1,0:T(8,128)(2,1)} async-done(((bf16[1,96,2496]{2,1,0:T(8,128)(2,1)}), bf16[1,768,2496]{2,1,0:T(8,128)(2,1)}) %all-gather.32.cloned.1.call-update) | async-done | bytes 3833872 | tf_op jit(solution)/shard_map/all_gather | solution.py:81
  83.0 6.3 copy.167
  89.3 86.7 %all-gather.22.cloned.1.call-done = bf16[3592,768]{0,1:T(8,128)(2,1)} async-done(((bf16[3592,96]{0,1:T(8,128)(2,1)}), bf16[3592,768]{0,1:T(8,128)(2,1)}) %all-gather.22.cloned.1.call-update) | async-done | bytes 5517328 | tf_op jit(solution)/shard_map/all_gather | solution.py:213
  186.7 5.2 all_gather.67
  200.4 20.6 %all-gather.34.cloned.1.call-done = bf16[1,960,768]{1,2,0:T(8,128)(2,1)} async-done(((bf16[1,960,96]{1,2,0:T(8,128)(2,1)}), bf16[1,960,768]{1,2,0:T(8,128)(2,1)}) %all-gather.34.cloned.1.call-update) | async-done | bytes 1474576 | tf_op jit(solution)/shard_map/all_gather | solution.py:82
  224.7 44.0 %all-gather.36.cloned.1.call-done = bf16[16,256,768]{2,1,0:T(8,128)(2,1)} async-done(((bf16[4,256,768]{2,1,0:T(8,128)(2,1)}), bf16[16,256,768]{2,1,0:T(8,128)(2,1)}) %all-gather.36.cloned.1.call-update) | async-done | bytes 6291472 | tf_op jit(solution)/shard_map/all_gather | solution.py:26
  268.7 5.3 reduce_sum.492
  287.1 53.8 %all-gather.38.cloned.1.call-done = bf16[1,768,2496]{2,1,0:T(8,128)(2,1)} async-done(((bf16[1,96,2496]{2,1,0:T(8,128)(2,1)}), bf16[1,768,2496]{2,1,0:T(8,128)(2,1)}) %all-gather.38.cloned.1.call-update) | async-done | bytes 3833872 | tf_op jit(solution)/shard_map/all_gather | solution.py:81
  340.9 6.2 copy.173
  349.4 5.6 all_gather.73
  356.2 31.9 %all-gather.24.cloned.1.call-done = bf16[4,4,256,768]{3,2,1,0:T(8,128)(2,1)} async-done(((bf16[1,4,256,768]{3,2,1,0:T(8,128)(2,1)}), bf16[4,4,256,768]{3,2,1,0:T(8,128)(2,1)}) %all-gather.24.cloned.1.call-update) | async-done | bytes 6291472 | tf_op jit(solution)/shard_map/all_gather | solution.py:26
  388.1 5.3 reduce_sum.498
  401.8 3.5 reshape.400
  411.4 23.5 %all-gather.40.cloned.1.call-done = bf16[1,960,768]{1,2,0:T(8,128)(2,1)} async-done(((bf16[1,960,96]{1,2,0:T(8,128)(2,1)}), bf16[1,960,768]{1,2,0:T(8,128)(2,1)}) %all-gather.40.cloned.1.call-update) | async-done | bytes 1474576 | tf_op jit(solution)/shard_map/all_gather | solution.py:82
  438.3 44.4 %all-gather.42.cloned.1.call-done = bf16[16,256,768]{2,1,0:T(8,128)(2,1)} async-done(((bf16[4,256,768]{2,1,0:T(8,128)(2,1)}), bf16[16,256,768]{2,1,0:T(8,128)(2,1)}) %all-gather.42.cloned.1.call-update) | async-done | bytes 6291472 | tf_op jit(solution)/shard_map/all_gather | solution.py:26
  482.6 5.3 reduce_sum.505
  496.2 3.4 convolution_convert_fusion.6
  503.0 43.1 %all-gather.26.cloned.1.call-done = bf16[4,4,256,768]{3,2,1,0:T(8,128)(2,1)} async-done(((bf16[1,4,256,768]{3,2,1,0:T(8,128)(2,1)}), bf16[4,4,256,768]{3,2,1,0:T(8,128)(2,1)}) %all-gather.26.cloned.1.call-update) | async-done | bytes 6291472 | tf_op jit(solution)/shard_map/all_gather | solution.py:26
  546.1 5.3 reduce_sum.511
  566.5 3.7 fusion.33
  570.2 4.4 convolution_convert_fusion.5
  574.9 46.3 %all-gather.28.cloned.1.call-done = bf16[4,4,256,768]{3,2,1,0:T(8,128)(2,1)} async-done(((bf16[1,4,256,768]{3,2,1,0:T(8,128)(2,1)}), bf16[4,4,256,768]{3,2,1,0:T(8,128)(2,1)}) %all-gather.28.cloned.1.call-update) | async-done | bytes 6291472 | tf_op jit(solution)/shard_map/all_gather | solution.py:26
  621.1 5.3 reduce_sum.524
  650.0 3.7 convolution_convert_fusion.3
  654.1 46.2 %all-gather.44.cloned.1.call-done = bf16[16,256,768]{2,1,0:T(8,128)(2,1)} async-done(((bf16[4,256,768]{2,1,0:T(8,128)(2,1)}), bf16[16,256,768]{2,1,0:T(8,128)(2,1)}) %all-gather.44.cloned.1.call-update) | async-done | bytes 6291472 | tf_op jit(solution)/shard_map/all_gather | solution.py:26
  700.3 5.3 reduce_sum.531
  718.3 3.7 fusion.26
  722.0 4.4 convolution_convert_fusion.4
  726.9 46.0 %all-gather.30.cloned.1.call-done = bf16[4,4,256,768]{3,2,1,0:T(8,128)(2,1)} async-done(((bf16[1,4,256,768]{3,2,1,0:T(8,128)(2,1)}), bf16[4,4,256,768]{3,2,1,0:T(8,128)(2,1)}) %all-gather.30.cloned.1.call-update) | async-done | bytes 6291472 | tf_op jit(solution)/shard_map/all_gather | solution.py:26
  772.9 5.3 reduce_sum.534
  798.7 3.9 convolution_convert_fusion.2
  803.2 3.9 fusion.160
  811.7 4.7 fusion.159
  829.8 8.4 concatenate.43
  839.6 4.4 fusion.183
  849.1 5.5 reduce_sum.541
  861.8 9.4 concatenate.42
  875.0 11.4 psum.22
  889.2 4.0 fusion.65
  904.8 12.3 copy.221
  922.1 4.7 reduce-scatter.20.cloned.1.call-done
  928.1 76.0 %reduce-scatter.18.cloned.1.call-done = f32[96,960]{1,0:T(8,128)} async-done(((f32[768,960]{1,0:T(8,128)}), f32[96,960]{1,0:T(8,128)}) %reduce-scatter.18.cloned.1.call-update) | async-done | bytes 368656
  1006.1 140.8 %reduce-scatter.14.cloned.1.call-done = f32[96,2496]{1,0:T(8,128)} async-done(((f32[768,2496]{1,0:T(8,128)}), f32[96,2496]{1,0:T(8,128)}) %reduce-scatter.14.cloned.1.call-update) | async-done | bytes 958480 | tf_op jit(solution)/shard_map/reduce_scatter | solution.py:262
  1146.9 142.8 %reduce-scatter.12.cloned.1.call-done = f32[96,2496]{1,0:T(8,128)} async-done(((f32[768,2496]{1,0:T(8,128)}), f32[96,2496]{1,0:T(8,128)}) %reduce-scatter.12.cloned.1.call-update) | async-done | bytes 958480 | tf_op jit(solution)/shard_map/reduce_scatter | solution.py:262
  1292.3 191.0 %reduce-scatter.16.cloned.1.call-done = f32[96,3592]{1,0:T(8,128)} async-done(((f32[768,3592]{1,0:T(8,128)}), f32[96,3592]{1,0:T(8,128)}) %reduce-scatter.16.cloned.1.call-update) | async-done | bytes 1379344
  1490.1 39.6 %all-reduce = (f32[]{:T(128)}, f32[]{:T(128)}) all-reduce(f32[]{:T(128)S(6)} %div.194, f32[]{:T(128)S(6)} %add.327), channel_id=1, replica_groups=mesh['dp'=8,'tensor'=4] {'dp','tensor'}, use_global_device_ids=true, to_apply=%region_20.21 | all-reduce | flops 2 | bytes 16 | tf_op jit(solution)/shard_map/psum | solution.py:287
  1530.4 3.6 fusion.161
  1541.1 6.9 fusion.163
  (546 shorter events, 220.3 us)
Async XLA Ops:
  7.2 75.8 %all-gather.32.cloned.1.call-start = ((), (), s32[]{:S(2)}) async-start(), calls=%async_computation.12 | async-start | bytes 4423680 | tf_op jit(solution)/shard_map/all_gather | solution.py:81
  10.0 165.9 %all-gather.22.cloned.1.call-start = ((), (), s32[]{:S(2)}) async-start(), calls=%async_computation.5 | async-start | bytes 6414336 | tf_op jit(solution)/shard_map/all_gather | solution.py:213
  11.1 210.0 %all-gather.34.cloned.1.call-start = ((), (), s32[]{:S(2)}) async-start(), calls=%async_computation.13 | async-start | bytes 1769472 | tf_op jit(solution)/shard_map/all_gather | solution.py:82
  12.0 256.8 %all-gather.36.cloned.1.call-start = ((), (), s32[]{:S(2)}) async-start(), calls=%async_computation.14 | async-start | bytes 7864320 | tf_op jit(solution)/shard_map/all_gather | solution.py:26
  12.3 165.5 %copy-start.152 = (bf16[4,128]{1,0:T(4,128)(2,1)}, bf16[4,128]{1,0:T(4,128)(2,1)S(1)}, u32[]{:S(2)}) copy-start(bf16[4,128]{1,0:T(4,128)(2,1)S(1)} %get-tuple-element.143) | copy-start | bytes 3076
  12.3 165.5 %copy-start.154 = (bf16[4,128]{1,0:T(4,128)(2,1)}, bf16[4,128]{1,0:T(4,128)(2,1)S(1)}, u32[]{:S(2)}) copy-start(bf16[4,128]{1,0:T(4,128)(2,1)S(1)} %get-tuple-element.144) | copy-start | bytes 3076
  12.4 163.5 %copy-start.105 = (bf16[4,256,16]{1,2,0:T(8,128)(2,1)}, bf16[4,256,16]{1,2,0:T(8,128)(2,1)S(1)}, u32[]{:S(2)}) copy-start(bf16[4,256,16]{1,2,0:T(8,128)(2,1)S(1)} %fusion.119) | copy-start | bytes 98308
  12.6 179.9 %copy-start.12 = (f32[256,768]{1,0:T(8,128)}, f32[256,768]{1,0:T(8,128)S(1)}, u32[]{:S(2)}) copy-start(f32[256,768]{1,0:T(8,128)S(1)} %pad_maximum_fusion.4) | copy-start | bytes 2359300
  89.3 92.8 %copy-start.158 = (s32[4]{0:T(128)S(1)}, s32[4]{0:T(128)}, u32[]{:S(2)}) copy-start(s32[4]{0:T(128)} %param.17) | copy-start | bytes 52
  175.9 9.0 copy-start.37
  177.7 14.8 copy-start.6
  177.7 16.0 %copy-start.117 = (f32[4,256]{1,0:T(4,128)}, f32[4,256]{1,0:T(4,128)S(1)}, u32[]{:S(2)}) copy-start(f32[4,256]{1,0:T(4,128)S(1)} %broadcast_multiply_fusion.4) | copy-start | bytes 12292
  186.7 7.1 copy-start.137
  200.4 73.6 %copy-start.53 = (bf16[4,3,64,256]{3,2,1,0:T(8,128)(2,1)}, bf16[4,3,64,256]{3,2,1,0:T(8,128)(2,1)S(1)}, u32[]{:S(2)}) copy-start(bf16[4,3,64,256]{3,2,1,0:T(8,128)(2,1)S(1)} %convolution_convert_fusion.15) | copy-start | bytes 1179652
  223.8 117.0 %all-gather.38.cloned.1.call-start = ((), (), s32[]{:S(2)}) async-start(), calls=%async_computation.15 | async-start | bytes 4423680 | tf_op jit(solution)/shard_map/all_gather | solution.py:81
  224.4 163.6 %all-gather.24.cloned.1.call-start = ((), (), s32[]{:S(2)}) async-start(), calls=%async_computation.6 | async-start | bytes 7864320 | tf_op jit(solution)/shard_map/all_gather | solution.py:26
  286.3 148.6 %all-gather.40.cloned.1.call-start = ((), (), s32[]{:S(2)}) async-start(), calls=%async_computation.16 | async-start | bytes 1769472 | tf_op jit(solution)/shard_map/all_gather | solution.py:82
  287.0 195.6 %all-gather.42.cloned.1.call-start = ((), (), s32[]{:S(2)}) async-start(), calls=%async_computation.17 | async-start | bytes 7864320 | tf_op jit(solution)/shard_map/all_gather | solution.py:26
  437.8 108.3 %all-gather.26.cloned.1.call-start = ((), (), s32[]{:S(2)}) async-start(), calls=%async_computation.7 | async-start | bytes 7864320 | tf_op jit(solution)/shard_map/all_gather | solution.py:26
  499.6 121.6 %all-gather.28.cloned.1.call-start = ((), (), s32[]{:S(2)}) async-start(), calls=%async_computation.8 | async-start | bytes 7864320 | tf_op jit(solution)/shard_map/all_gather | solution.py:26
  554.3 6.8 copy-start.4
  554.4 6.8 copy-start.97
  554.9 6.3 copy-start.115
  564.1 6.1 copy-start.68
  574.6 125.6 %all-gather.44.cloned.1.call-start = ((), (), s32[]{:S(2)}) async-start(), calls=%async_computation.18 | async-start | bytes 7864320 | tf_op jit(solution)/shard_map/all_gather | solution.py:26
  653.8 119.2 %all-gather.30.cloned.1.call-start = ((), (), s32[]{:S(2)}) async-start(), calls=%async_computation.9 | async-start | bytes 7864320 | tf_op jit(solution)/shard_map/all_gather | solution.py:26
  714.2 7.8 copy-start.18
  714.5 7.5 copy-start.70
  726.4 122.7 %all-gather.46.cloned.1.call-start = ((), (), s32[]{:S(2)}) async-start(), calls=%async_computation.19 | async-start | bytes 7864320 | tf_op jit(solution)/shard_map/all_gather | solution.py:26
  786.7 6.0 copy-start.9
  802.6 124.3 %reduce-scatter.20.cloned.1.call-start = ((), (), s32[]{:S(2)}) async-start(), calls=%async_computation.22 | async-start | bytes 3538944
  810.1 193.9 %reduce-scatter.18.cloned.1.call-start = ((), (), s32[]{:S(2)}) async-start(), calls=%async_computation.21 | async-start | bytes 3538944
  819.6 327.4 %reduce-scatter.14.cloned.1.call-start = ((), (), s32[]{:S(2)}) async-start(), calls=%async_computation.11 | async-start | bytes 8847360 | tf_op jit(solution)/shard_map/reduce_scatter | solution.py:262
  838.2 5.7 copy-start.36
  838.2 451.5 %reduce-scatter.12.cloned.1.call-start = ((), (), s32[]{:S(2)}) async-start(), calls=%async_computation.10 | async-start | bytes 8847360 | tf_op jit(solution)/shard_map/reduce_scatter | solution.py:262
  849.1 5.5 copy-start.7
  849.1 5.5 copy-start.96
  849.1 5.5 copy-start.118
  871.2 15.2 copy-start.139
  871.2 15.2 copy-start.140
  871.2 17.9 %copy-start.106 = (bf16[4,256,16]{1,2,0:T(8,128)(2,1)S(1)}, bf16[4,256,16]{1,2,0:T(8,128)(2,1)}, u32[]{:S(2)}) copy-start(bf16[4,256,16]{1,2,0:T(8,128)(2,1)} %copy-done.105) | copy-start | bytes 98308
  871.3 612.0 %reduce-scatter.16.cloned.1.call-start = ((), (), s32[]{:S(2)}) async-start(), calls=%async_computation.20 | async-start | bytes 12828672
  1534.0 5.8 copy-start.42
  1534.0 7.1 copy-start.38
  1541.1 6.9 copy-start.40
  1541.1 6.9 copy-start.41
  1541.1 6.9 copy-start.72
  1541.1 6.9 copy-start.73
  (139 other events, 352.5 us)
Sparse Core Ops, SparseCore 0:
  10.8 72.1 all-gather.31
  85.8 90.1 all-gather.21
  178.7 42.3 all-gather.33
  224.0 44.7 all-gather.35
  271.3 69.4 all-gather.37
  342.9 45.1 all-gather.23
  390.8 43.9 all-gather.39
  437.9 44.7 all-gather.41
  499.7 46.3 all-gather.25
  574.8 46.3 all-gather.27
  653.9 46.3 all-gather.43
  726.5 46.3 all-gather.29
  802.7 46.3 all-gather.45
  852.5 74.2 reduce-scatter.19
  930.3 73.7 reduce-scatter.17
  1007.6 139.3 reduce-scatter.13
  1150.4 139.2 reduce-scatter.11
  1293.3 189.9 reduce-scatter.15
